TPU v7x, 32 devices: a whole 2x2x4 slice. The times are simulated.
32 devices in a mesh: dp: 8 (over z, core), mp: 4 (over y, x).
Axes of the slice: x: 2, y: 2, z: 4, core: 2. Of those that a mesh axis runs over, the one named last changes fastest.
Arguments:
- token_ids: int32 [8192], P('dp'), may hold values from 0 to 128255
- lengths: int32 [64], P('dp'), may hold values from 1 to 128
- embed_grads: bfloat16 [8192, 4096], P('dp', 'mp'), may hold values from -6 to 6
- vocab_basis: bfloat16 [128256, 32], P('mp'), may hold values from -6 to 6
- embed_basis: bfloat16 [4096, 32], P('mp'), may hold values from -0.09375 to 0.09375
- layer_inputs: bfloat16 [1, 8192, 4096], P(None, 'dp', 'mp'), may hold values from -6 to 6
- layer_grads: bfloat16 [1, 8192, 4096], P(None, 'dp', 'mp'), may hold values from -6 to 6
- input_basis: bfloat16 [1, 4096, 32], P(None, 'mp'), may hold values from -0.09375 to 0.09375
- output_basis: bfloat16 [1, 4096, 32], P(None, 'mp'), may hold values from -0.09375 to 0.09375
- queries: bfloat16 [2, 1024, 256], P(None, 'mp', 'dp'), may hold values from -0.19921875 to 0.19921875
Outputs:
- scores: float32 [64, 256], P('dp')
All inputs are finite; a program needn't handle non-finite values.
Results may differ from a plain program's by a relative error of at most 0.0003.
Values may be sent and summed in bfloat16 or wider, within the bound.
No kernel may reach another device: no remote copies, remote signals or barrier semaphores. Data moves between devices by JAX's collectives and lax.ppermute only.
A program may use at most 64 MiB of HBM per device.

v0:
```python
import jax
import jax.numpy as jnp
from jax import lax
from jax.sharding import PartitionSpec as P

ITERS = 2
damping = 0.01
epsilon = 1e-06
highest = lax.Precision.HIGHEST


def solve_columns(right_side, apply_operator, column_norm, column_curve):
    solution = jnp.zeros_like(right_side)
    residual = right_side
    direction = right_side
    norm_now = column_norm(residual)
    for iteration in range(ITERS):
        images = apply_operator(direction)
        step_size = norm_now / (column_curve(direction, images) + epsilon)
        solution = solution + step_size[:, None, :] * direction
        residual = residual - step_size[:, None, :] * images
        norm_next = column_norm(residual)
        direction = residual + (norm_next / (norm_now + epsilon))[:, None, :] * direction
        norm_now = norm_next
    return solution


def per_device(
    token_ids,
    lengths,
    embed_grads,
    vocab_basis,
    embed_basis,
    layer_inputs,
    layer_grads,
    input_basis,
    output_basis,
    queries,
):
    vocab_rows = vocab_basis.shape[0]
    basis_rank = embed_basis.shape[1]
    layer_count = layer_inputs.shape[0] + 1
    seq_count = lengths.shape[0]
    token_count = token_ids.shape[0]
    slot_len = token_count // seq_count
    sketch_len = basis_rank * basis_rank
    mp_index = lax.axis_index("mp")
    local_ids = token_ids - mp_index * vocab_rows
    inside = (local_ids >= 0) & (local_ids < vocab_rows)
    looked = jnp.take(vocab_basis, jnp.clip(local_ids, 0, vocab_rows - 1), axis=0)
    pieces = [
        jnp.dot(embed_grads, embed_basis, preferred_element_type=jnp.float32),
        jnp.where(inside[:, None], looked.astype(jnp.float32), 0.0),
    ]
    pieces.append(jnp.dot(layer_grads[0], output_basis[0], preferred_element_type=jnp.float32))
    pieces.append(jnp.dot(layer_inputs[0], input_basis[0], preferred_element_type=jnp.float32))
    projected = jnp.concatenate(pieces, axis=1)
    inverse_len = 1.0 / lengths.astype(jnp.float32)
    summed = lax.psum(projected, "mp")
    layout = summed.reshape(seq_count, slot_len, layer_count, 2, basis_rank)
    position = jnp.arange(slot_len, dtype=jnp.int32)
    weights = jnp.where(position[None, :] < lengths[:, None], inverse_len[:, None], 0.0)
    weighted = layout[:, :, :, 0, :] * weights[:, :, None, None]
    sketches = jnp.einsum(
        "stli,stlj->lsij", weighted, layout[:, :, :, 1, :], precision=highest
    ).reshape(layer_count, seq_count, sketch_len)
    examples = seq_count * lax.axis_size("dp")
    targets = lax.all_gather(queries, "dp", axis=2, tiled=True)
    everyone = lax.all_gather(sketches, "dp", axis=1, tiled=True)
    columns = lax.all_to_all(targets, "mp", split_axis=2, concat_axis=1, tiled=True)

    def apply_sketch(direction):
        inner_sums = jnp.einsum("lek,lkq->leq", everyone, direction, precision=highest)
        back_proj = jnp.einsum("lek,leq->lkq", everyone, inner_sums, precision=highest)
        return back_proj / examples + damping * direction

    def local_norm(residual):
        return jnp.sum(residual * residual, axis=1)

    def local_curve(direction, images):
        return jnp.sum(direction * images, axis=1)

    solution = solve_columns(columns.astype(jnp.float32), apply_sketch, local_norm, local_curve)
    partial_value = jnp.einsum("lek,lkq->eq", sketches, solution, precision=highest)
    scores = lax.all_gather(partial_value, "mp", axis=1, tiled=True)
    return scores


def solution(mesh):
    placed = (
        P("dp"),
        P("dp"),
        P("dp", "mp"),
        P("mp", None),
        P("mp", None),
        P(None, "dp", "mp"),
        P(None, "dp", "mp"),
        P(None, "mp", None),
        P(None, "mp", None),
        P(None, "mp", "dp"),
    )
    return jax.shard_map(
        per_device, mesh=mesh, in_specs=placed, out_specs=P("dp", None), check_vma=False
    )
```

profile of v0, /device:TPU:0, one launch (start us, length us, event | category | flops | bytes accessed | tf_op | source)
XLA Modules:
  0.0 111.8 jit_solution(4883537781208353662)
XLA Ops:
  6.5 0.0 copy-start
  6.5 0.0 all-reduce.2.cloned.1.call-start
  6.5 0.8 compare_and_fusion.1
  7.4 0.7 fusion.25
  8.1 7.3 %copy.30 = bf16[32064,32]{1,0:T(8,128)(2,1)} copy(bf16[32064,32]{0,1:T(8,128)(2,1)} %param.13) | data formatting | bytes 4104192 | tf_op args[3]
  15.4 0.0 copy-start.3
  15.4 0.0 copy-start.4
  15.4 7.3 %gather_fusion = bf16[1024,32]{1,0:T(8,128)(2,1)S(1)} fusion(bf16[32064,32]{1,0:T(8,128)(2,1)} %copy.30, s32[1024]{0:T(1024)S(1)} %fusion.25), kind=kCustom, calls=%fused_computation | custom fusion | bytes 135168 | tf_op jit(solution)/shard_map/jit(_take)/gather | solution.py:50
  22.7 0.1 copy.31
  22.8 0.0 copy-done
  22.8 0.0 copy-done.3
  22.8 0.0 copy-start.1
  22.8 0.0 copy-start.2
  22.8 0.0 copy-start.5
  22.8 0.7 fusion
  23.6 0.0 copy-done.4
  23.6 0.8 copy-done.1
  24.4 0.7 fusion.2
  25.1 0.0 copy-done.2
  25.1 0.0 copy-done.5
  25.1 0.7 fusion.26
  25.9 0.0 copy-start.6
  25.9 0.0 copy-start.7
  26.0 0.1 copy.38
  26.1 0.9 copy.32
  27.0 0.0 all-reduce.2.cloned.1.call-update
  27.0 0.0 copy-done.6
  27.0 17.0 %all_gather.9 = bf16[2,256,256]{1,0,2:T(2,128)(2,1)} all-gather(bf16[2,256,32]{1,0,2:T(2,128)(2,1)S(1)} %copy.28), channel_id=1, replica_groups=mesh['dp'=8,'mp'=4] {'dp'}, dimensions={2}, use_global_device_ids=true | all-gather | bytes 294912 | tf_op jit(solution)/shard_map/all_gather | solution.py:68
  44.0 3.7 %all-to-all-start = ((bf16[2,256,256]{1,0,2:T(2,128)(2,1)}), bf16[2,256,256]{1,0,2:T(2,128)(2,1)S(1)}, u32[]{:S(2)}, u32[]{:S(2)}) async-start(bf16[2,256,256]{1,0,2:T(2,128)(2,1)} %all_gather.9), calls=%async_computation | async-start | bytes 524288 | tf_op jit(solution)/shard_map/all_to_all | solution.py:70
  47.7 0.0 copy-done.7
  47.8 0.1 fusion.24
  47.8 5.8 %all-to-all-done = bf16[2,256,256]{1,0,2:T(2,128)(2,1)S(1)} async-done(((bf16[2,256,256]{1,0,2:T(2,128)(2,1)}), bf16[2,256,256]{1,0,2:T(2,128)(2,1)S(1)}, u32[]{:S(2)}, u32[]{:S(2)}) %all-to-all-start) | async-done | bytes 262176 | tf_op jit(solution)/shard_map/all_to_all | solution.py:70
  53.6 0.2 copy.42
  53.8 0.2 all_to_all.16
  54.0 0.6 multiply_reduce_fusion.1
  54.6 21.5 %all-reduce.2.cloned.1.call-done = f32[8,128,2,2,32]{1,4,0,2,3:T(8,128)} async-done(((f32[8,128,2,2,32]{1,4,0,2,3:T(8,128)}), f32[8,128,2,2,32]{1,4,0,2,3:T(8,128)}) %all-reduce.2.cloned.1.call-update) | async-done | bytes 524304 | tf_op jit(solution)/shard_map/psum | solution.py:59
  76.0 1.6 %fusion.13 = f32[2,8,32,32]{3,2,1,0:T(8,128)S(1)} fusion(f32[8,128,2,2,32]{1,4,0,2,3:T(8,128)} %all-reduce.2.cloned.1.call-done, f32[8,128]{1,0:T(8,128)S(1)} %fusion.24), kind=kOutput, calls=%fused_computation.25 | convolution fusion | flops 25231360 | bytes 593920 | tf_op jit(solution)/shard_map/stli,stlj->lsij/dot_general | solution.py:64
  77.6 0.1 reshape.68
  77.7 14.7 %all_gather.10 = f32[2,64,1024]{2,1,0:T(8,128)S(1)} all-gather(f32[2,8,1024]{2,1,0:T(8,128)S(1)} %reshape.68), channel_id=1, replica_groups=mesh['dp'=8,'mp'=4] {'dp'}, dimensions={1}, use_global_device_ids=true | all-gather | bytes 589824 | tf_op jit(solution)/shard_map/all_gather | solution.py:69
  92.4 0.4 fusion.27
  92.9 0.8 fusion.8
  93.7 0.2 multiply_reduce_fusion
  93.9 0.7 fusion.19
  94.6 0.8 fusion.7
  95.4 0.7 convolution_bitcast_fusion
  96.1 8.1 %all-gather = f32[4,64,8]{1,2,0:T(8,128)S(1)} all-gather(f32[1,64,8]{1,2,0:T(8,128)S(1)} %convolution_bitcast_fusion), channel_id=1, replica_groups=mesh['dp'=8,'mp'=4] {'mp'}, dimensions={0}, use_global_device_ids=true | all-gather | bytes 10240 | tf_op jit(solution)/shard_map/all_gather | solution.py:85
  104.3 0.7 reshape.79
  (8 shorter events, 0.1 us)
Async XLA Ops:
  6.5 16.2 %copy-start = (bf16[1,1024,1024]{2,1,0:T(8,128)(2,1)S(1)}, bf16[1,1024,1024]{2,1,0:T(8,128)(2,1)}, u32[]{:S(2)}) copy-start(bf16[1,1024,1024]{2,1,0:T(8,128)(2,1)} %param.15) | copy-start | bytes 6291460
  6.5 69.5 %all-reduce.2.cloned.1.call-start = ((), (), s32[]{:S(2)}) async-start(), calls=%async_computation.1 | async-start | bytes 1048576 | tf_op jit(solution)/shard_map/psum | solution.py:59
  15.4 7.4 %copy-start.3 = (bf16[1,1024,32]{1,2,0:T(8,128)(2,1)S(1)}, bf16[1,1024,32]{1,2,0:T(8,128)(2,1)}, u32[]{:S(2)}) copy-start(bf16[1,1024,32]{1,2,0:T(8,128)(2,1)} %param.17) | copy-start | bytes 196612
  15.4 8.2 %copy-start.4 = (bf16[1,1024,32]{1,2,0:T(8,128)(2,1)S(1)}, bf16[1,1024,32]{1,2,0:T(8,128)(2,1)}, u32[]{:S(2)}) copy-start(bf16[1,1024,32]{1,2,0:T(8,128)(2,1)} %param.18) | copy-start | bytes 196612
  22.8 1.6 %copy-start.1 = (bf16[1,1024,1024]{2,1,0:T(8,128)(2,1)S(1)}, bf16[1,1024,1024]{2,1,0:T(8,128)(2,1)}, u32[]{:S(2)}) copy-start(bf16[1,1024,1024]{2,1,0:T(8,128)(2,1)} %param.16) | copy-start | bytes 6291460
  22.8 2.3 %copy-start.2 = (bf16[1024,1024]{1,0:T(8,128)(2,1)S(1)}, bf16[1024,1024]{1,0:T(8,128)(2,1)}, u32[]{:S(2)}) copy-start(bf16[1024,1024]{1,0:T(8,128)(2,1)} %param.12) | copy-start | bytes 6291460
  22.8 2.3 %copy-start.5 = (bf16[1024,32]{0,1:T(8,128)(2,1)S(1)}, bf16[1024,32]{0,1:T(8,128)(2,1)}, u32[]{:S(2)}) copy-start(bf16[1024,32]{0,1:T(8,128)(2,1)} %param.14) | copy-start | bytes 196612
  25.9 1.1 %copy-start.6 = (bf16[2,256,32]{1,2,0:T(8,128)(2,1)S(1)}, bf16[2,256,32]{1,2,0:T(8,128)(2,1)}, u32[]{:S(2)}) copy-start(bf16[2,256,32]{1,2,0:T(8,128)(2,1)} %param.19) | copy-start | bytes 98308
  25.9 21.9 %copy-start.7 = (s32[8]{0:T(128)S(1)}, s32[8]{0:T(128)}, u32[]{:S(2)}) copy-start(s32[8]{0:T(128)} %param.11) | copy-start | bytes 100
  44.0 9.6 %all-to-all-start = ((bf16[2,256,256]{1,0,2:T(2,128)(2,1)}), bf16[2,256,256]{1,0,2:T(2,128)(2,1)S(1)}, u32[]{:S(2)}, u32[]{:S(2)}) async-start(bf16[2,256,256]{1,0,2:T(2,128)(2,1)} %all_gather.9), calls=%async_computation | async-start | bytes 524288 | tf_op jit(solution)/shard_map/all_to_all | solution.py:70
Sparse Core Ops, SparseCore 0:
  27.1 48.8 all-reduce.1
where the time goes:
time: 112 us
  blocking collectives  39.8 us (36%)
  waiting for transfers between devices  27.3 us (24%)
  local copies, waits for them, and re-layouts  17.8 us (16%)
  between operations  13.6 us (12%)
  matrix products  7.11 us (6%)
  starting transfers between devices  3.71 us (3%)
  other arithmetic  2.52 us (2%)
    psum x1, waiting for transfers between devices, per_device(): summed = lax.psum(projected, 'mp')  21.5 us
    all_gather x1, blocking collectives, per_device(): targets = lax.all_gather(queries, 'dp', axis=2, tiled=True)  17 us
    all_gather x1, blocking collectives, per_device(): everyone = lax.all_gather(sketches, 'dp', axis=1, tiled=True)  14.7 us
    unnamed x20, local copies, waits for them, and re-layouts  8.96 us
    all_gather x1, blocking collectives, per_device(): scores = lax.all_gather(partial_value, 'mp', axis=1, tiled=True)  8.14 us
    gather x2, local copies, waits for them, and re-layouts, per_device(): jnp.take(vocab_basis, jnp.clip(local_ids, 0, vocab_rows - 1), axis=0)  7.42 us
    all_to_all x1, waiting for transfers between devices, per_device(): lax.all_to_all(targets, 'mp', split_axis=2, concat_axis=1, tiled=True)  5.79 us
    all_to_all x1, starting transfers between devices, per_device(): lax.all_to_all(targets, 'mp', split_axis=2, concat_axis=1, tiled=True)  3.71 us
  transfers between devices with their start and end apart: 2, of which 2 were waited for; matrix products, arithmetic and copies ran while one was open for 1% of the time, Pallas kernels for 0%

commit v1 on v0

--- a/solution.py
+++ b/solution.py
@@ -56,7 +56,10 @@
     pieces.append(jnp.dot(layer_inputs[0], input_basis[0], preferred_element_type=jnp.float32))
     projected = jnp.concatenate(pieces, axis=1)
     inverse_len = 1.0 / lengths.astype(jnp.float32)
-    summed = lax.psum(projected, "mp")
+    size, summed = (lax.axis_size("mp"), projected)
+    for hop in [1 << k for k in range(size.bit_length() - 1)]:
+        swap = [(i, i ^ hop) for i in range(size)]
+        summed = summed + lax.ppermute(summed, "mp", swap)
     layout = summed.reshape(seq_count, slot_len, layer_count, 2, basis_rank)
     position = jnp.arange(slot_len, dtype=jnp.int32)
     weights = jnp.where(position[None, :] < lengths[:, None], inverse_len[:, None], 0.0)

time: 112 us -> 88.5 us (0.79)
  waiting for transfers between devices: 27.3 us -> 13.1 us
  between operations: 13.6 us -> 0.2 us
  starting transfers between devices: 3.71 us -> 8.48 us
  other arithmetic: 2.52 us -> 4.72 us
  blocking collectives: 39.8 us -> 38.5 us
    psum x1 -> x0, waiting for transfers between devices: 21.5 us -> none  [per_device(): summed = lax.psum(projected, 'mp')]
    ppermute x0 -> x2, waiting for transfers between devices: none -> 9.99 us  [per_device(): summed = summed + lax.ppermute(summed, 'mp', swap)]
    ppermute x0 -> x2, starting transfers between devices: none -> 5.08 us  [per_device(): summed = summed + lax.ppermute(summed, 'mp', swap)]
    all_to_all x1, waiting for transfers between devices: 5.79 us -> 3.09 us  [per_device(): lax.all_to_all(targets, 'mp', split_axis=2, concat_axis=1, tiled=True)]
    all_gather x1, blocking collectives: 17 us -> 15.5 us  [per_device(): targets = lax.all_gather(queries, 'dp', axis=2, tiled=True)]
  transfers between devices with their start and end apart: 2 -> 3, of which waited for: 2 -> 2; matrix products, arithmetic and copies ran while one was open for 1% -> 2% of each run, Pallas kernels for 0% -> 0%
where the time goes in v1:
time: 88.5 us; the launch traced here: 88.1 us
  blocking collectives  38.5 us (44%)
  local copies, waits for them, and re-layouts  16.9 us (19%)
  waiting for transfers between devices  13.1 us (15%)
  starting transfers between devices  8.48 us (10%)
  matrix products  6.13 us (7%)
  other arithmetic  4.72 us (5%)
    all_gather x1, blocking collectives, per_device(): targets = lax.all_gather(queries, 'dp', axis=2, tiled=True)  15.5 us
    all_gather x1, blocking collectives, per_device(): everyone = lax.all_gather(sketches, 'dp', axis=1, tiled=True)  14.8 us
    ppermute x2, waiting for transfers between devices, per_device(): summed = summed + lax.ppermute(summed, 'mp', swap)  9.99 us
    unnamed x20, local copies, waits for them, and re-layouts  8.97 us
    all_gather x1, blocking collectives, per_device(): scores = lax.all_gather(partial_value, 'mp', axis=1, tiled=True)  8.14 us
    gather x2, local copies, waits for them, and re-layouts, per_device(): jnp.take(vocab_basis, jnp.clip(local_ids, 0, vocab_rows - 1), axis=0)  7.42 us
    ppermute x2, starting transfers between devices, per_device(): summed = summed + lax.ppermute(summed, 'mp', swap)  5.08 us
    all_to_all x1, starting transfers between devices, per_device(): lax.all_to_all(targets, 'mp', split_axis=2, concat_axis=1, tiled=True)  3.4 us
  transfers between devices with their start and end apart: 3, of which 2 were waited for; matrix products, arithmetic and copies ran while one was open for 2% of the time, Pallas kernels for 0%

profile of v1, /device:TPU:0, one launch (start us, length us, event | category | flops | bytes accessed | tf_op | source)
XLA Modules:
  0.0 88.1 jit_solution(1406758532717162953)
XLA Ops:
  0.0 0.0 copy-start
  0.0 0.8 compare_and_fusion.1
  0.8 0.7 fusion.25
  1.5 7.3 %copy.33 = bf16[32064,32]{1,0:T(8,128)(2,1)} copy(bf16[32064,32]{0,1:T(8,128)(2,1)} %param.13) | data formatting | bytes 4104192 | tf_op args[3]
  8.8 0.0 copy-start.3
  8.8 0.0 copy-start.4
  8.8 7.3 %gather_fusion = bf16[1024,32]{1,0:T(8,128)(2,1)S(1)} fusion(bf16[32064,32]{1,0:T(8,128)(2,1)} %copy.33, s32[1024]{0:T(1024)S(1)} %fusion.25), kind=kCustom, calls=%fused_computation | custom fusion | bytes 135168 | tf_op jit(solution)/shard_map/jit(_take)/gather | solution.py:50
  16.1 0.1 copy.34
  16.2 0.0 copy-done
  16.3 0.0 copy-done.3
  16.3 0.0 copy-start.1
  16.3 0.0 copy-start.2
  16.3 0.0 copy-start.5
  16.3 0.7 fusion
  17.0 0.0 copy-done.4
  17.0 0.8 copy-done.1
  17.9 0.7 fusion.2
  18.6 0.0 copy-done.2
  18.6 0.0 copy-done.5
  18.6 0.0 copy-start.6
  18.6 0.7 fusion.28
  19.3 0.0 copy-start.7
  19.4 3.0 %collective-permute-start = (f32[1024,128]{0,1:T(8,128)S(1)}, f32[1024,128]{0,1:T(8,128)}, u32[]{:S(2)}, u32[]{:S(2)}) collective-permute-start(f32[1024,128]{0,1:T(8,128)S(1)} %pad_maximum_fusion), channel_id=1, source_target_pairs={{0,1},{1,0},{2,3},{3,2},{4,5},{5,4},{6,7},{7,6},{8,9},{9,8},{10,11... | collective-permute-start | bytes 1572872 | tf_op jit(solution)/shard_map/ppermute | solution.py:62
  22.5 0.0 copy-done.6
  22.5 15.5 %all_gather.9 = bf16[2,256,256]{1,0,2:T(2,128)(2,1)} all-gather(bf16[2,256,32]{1,0,2:T(2,128)(2,1)S(1)} %copy.31), channel_id=1, replica_groups=mesh['dp'=8,'mp'=4] {'dp'}, dimensions={2}, use_global_device_ids=true | all-gather | bytes 294912 | tf_op jit(solution)/shard_map/all_gather | solution.py:71
  38.0 3.4 %all-to-all-start = ((bf16[2,256,256]{1,0,2:T(2,128)(2,1)}), bf16[2,256,256]{1,0,2:T(2,128)(2,1)S(1)}, u32[]{:S(2)}, u32[]{:S(2)}) async-start(bf16[2,256,256]{1,0,2:T(2,128)(2,1)} %all_gather.9), calls=%async_computation | async-start | bytes 524288 | tf_op jit(solution)/shard_map/all_to_all | solution.py:73
  41.4 0.0 collective-permute-done
  41.4 1.1 %fusion.26 = f32[1024,128]{0,1:T(8,128)S(1)} fusion(f32[1024,128]{0,1:T(8,128)} %collective-permute-done, f32[1024,32]{0,1:T(8,128)S(1)} %fusion, f32[1024,32]{0,1:T(8,128)S(1)} %fusion.2, f32[1024,32]{0,1:T(8,128)S(1)} %convert_select_fusion, f32[1024,32]{0,1:T(8,128)S(1)} %fusion.28), kind=kLoop, calls=%fused_computation.47 | loop fusion | flops 524288 | bytes 1572864 | tf_op jit(solution)/shard_map/add | solution.py:62
  42.5 2.0 %collective-permute-start.1 = (f32[1024,128]{0,1:T(8,128)S(1)}, f32[1024,128]{0,1:T(8,128)}, u32[]{:S(2)}, u32[]{:S(2)}) collective-permute-start(f32[1024,128]{0,1:T(8,128)S(1)} %fusion.26), channel_id=1, source_target_pairs={{0,2},{1,3},{2,0},{3,1},{4,6},{5,7},{6,4},{7,5},{8,10},{9,11},{10,... | collective-permute-start | bytes 1572872 | tf_op jit(solution)/shard_map/ppermute | solution.py:62
  44.6 0.0 copy-done.7
  44.6 0.1 fusion.24
  44.7 3.1 %all-to-all-done = bf16[2,256,256]{1,0,2:T(2,128)(2,1)S(1)} async-done(((bf16[2,256,256]{1,0,2:T(2,128)(2,1)}), bf16[2,256,256]{1,0,2:T(2,128)(2,1)S(1)}, u32[]{:S(2)}, u32[]{:S(2)}) %all-to-all-start) | async-done | bytes 262176 | tf_op jit(solution)/shard_map/all_to_all | solution.py:73
  47.8 0.2 copy.54
  48.0 0.2 all_to_all.16
  48.1 0.6 multiply_reduce_fusion.1
  48.7 10.0 %collective-permute-done.1 = f32[1024,128]{0,1:T(8,128)} collective-permute-done((f32[1024,128]{0,1:T(8,128)S(1)}, f32[1024,128]{0,1:T(8,128)}, u32[]{:S(2)}, u32[]{:S(2)}) %collective-permute-start.1) | collective-permute-done | bytes 524320 | tf_op jit(solution)/shard_map/ppermute | solution.py:62
  58.7 1.1 %add_bitcast_fusion = f32[16,8,8,128]{3,1,2,0:T(8,128)S(1)} fusion(f32[1024,128]{0,1:T(8,128)S(1)} %fusion.26, f32[1024,128]{0,1:T(8,128)} %collective-permute-done.1), kind=kLoop, calls=%fused_computation.24 | loop fusion | flops 131072 | bytes 1572864
  59.8 0.1 copy.44
  59.9 0.6 fusion.13
  60.5 0.1 reshape.68
  60.7 14.8 %all_gather.10 = f32[2,64,1024]{2,1,0:T(8,128)S(1)} all-gather(f32[2,8,1024]{2,1,0:T(8,128)S(1)} %reshape.68), channel_id=1, replica_groups=mesh['dp'=8,'mp'=4] {'dp'}, dimensions={1}, use_global_device_ids=true | all-gather | bytes 589824 | tf_op jit(solution)/shard_map/all_gather | solution.py:72
  75.5 0.4 fusion.29
  75.9 0.8 fusion.8
  76.7 0.2 multiply_reduce_fusion
  77.0 0.7 fusion.19
  77.7 0.8 fusion.7
  78.5 0.7 convolution_bitcast_fusion
  79.2 8.1 %all-gather = f32[4,64,8]{1,2,0:T(8,128)S(1)} all-gather(f32[1,64,8]{1,2,0:T(8,128)S(1)} %convolution_bitcast_fusion), channel_id=1, replica_groups=mesh['dp'=8,'mp'=4] {'mp'}, dimensions={0}, use_global_device_ids=true | all-gather | bytes 10240 | tf_op jit(solution)/shard_map/all_gather | solution.py:88
  87.4 0.7 reshape.79
  (9 shorter events, 0.2 us)
Async XLA Ops:
  0.0 16.2 %copy-start = (bf16[1,1024,1024]{2,1,0:T(8,128)(2,1)S(1)}, bf16[1,1024,1024]{2,1,0:T(8,128)(2,1)}, u32[]{:S(2)}) copy-start(bf16[1,1024,1024]{2,1,0:T(8,128)(2,1)} %param.15) | copy-start | bytes 6291460
  8.8 7.4 %copy-start.3 = (bf16[1,1024,32]{1,2,0:T(8,128)(2,1)S(1)}, bf16[1,1024,32]{1,2,0:T(8,128)(2,1)}, u32[]{:S(2)}) copy-start(bf16[1,1024,32]{1,2,0:T(8,128)(2,1)} %param.17) | copy-start | bytes 196612
  8.8 8.2 %copy-start.4 = (bf16[1,1024,32]{1,2,0:T(8,128)(2,1)S(1)}, bf16[1,1024,32]{1,2,0:T(8,128)(2,1)}, u32[]{:S(2)}) copy-start(bf16[1,1024,32]{1,2,0:T(8,128)(2,1)} %param.18) | copy-start | bytes 196612
  16.3 1.6 %copy-start.1 = (bf16[1,1024,1024]{2,1,0:T(8,128)(2,1)S(1)}, bf16[1,1024,1024]{2,1,0:T(8,128)(2,1)}, u32[]{:S(2)}) copy-start(bf16[1,1024,1024]{2,1,0:T(8,128)(2,1)} %param.16) | copy-start | bytes 6291460
  16.3 2.3 %copy-start.2 = (bf16[1024,1024]{1,0:T(8,128)(2,1)S(1)}, bf16[1024,1024]{1,0:T(8,128)(2,1)}, u32[]{:S(2)}) copy-start(bf16[1024,1024]{1,0:T(8,128)(2,1)} %param.12) | copy-start | bytes 6291460
  16.3 2.3 %copy-start.5 = (bf16[1024,32]{0,1:T(8,128)(2,1)S(1)}, bf16[1024,32]{0,1:T(8,128)(2,1)}, u32[]{:S(2)}) copy-start(bf16[1024,32]{0,1:T(8,128)(2,1)} %param.14) | copy-start | bytes 196612
  18.6 3.9 %copy-start.6 = (bf16[2,256,32]{1,2,0:T(8,128)(2,1)S(1)}, bf16[2,256,32]{1,2,0:T(8,128)(2,1)}, u32[]{:S(2)}) copy-start(bf16[2,256,32]{1,2,0:T(8,128)(2,1)} %param.19) | copy-start | bytes 98308
  19.3 25.3 %copy-start.7 = (s32[8]{0:T(128)S(1)}, s32[8]{0:T(128)}, u32[]{:S(2)}) copy-start(s32[8]{0:T(128)} %param.11) | copy-start | bytes 100
  19.4 22.0 %collective-permute-start = (f32[1024,128]{0,1:T(8,128)S(1)}, f32[1024,128]{0,1:T(8,128)}, u32[]{:S(2)}, u32[]{:S(2)}) collective-permute-start(f32[1024,128]{0,1:T(8,128)S(1)} %pad_maximum_fusion), channel_id=1, source_target_pairs={{0,1},{1,0},{2,3},{3,2},{4,5},{5,4},{6,7},{7,6},{8,9},{9,8},{10,11... | collective-permute-start | bytes 1572872 | tf_op jit(solution)/shard_map/ppermute | solution.py:62
  38.0 9.7 %all-to-all-start = ((bf16[2,256,256]{1,0,2:T(2,128)(2,1)}), bf16[2,256,256]{1,0,2:T(2,128)(2,1)S(1)}, u32[]{:S(2)}, u32[]{:S(2)}) async-start(bf16[2,256,256]{1,0,2:T(2,128)(2,1)} %all_gather.9), calls=%async_computation | async-start | bytes 524288 | tf_op jit(solution)/shard_map/all_to_all | solution.py:73
  42.5 16.1 %collective-permute-start.1 = (f32[1024,128]{0,1:T(8,128)S(1)}, f32[1024,128]{0,1:T(8,128)}, u32[]{:S(2)}, u32[]{:S(2)}) collective-permute-start(f32[1024,128]{0,1:T(8,128)S(1)} %fusion.26), channel_id=1, source_target_pairs={{0,2},{1,3},{2,0},{3,1},{4,6},{5,7},{6,4},{7,5},{8,10},{9,11},{10,... | collective-permute-start | bytes 1572872 | tf_op jit(solution)/shard_map/ppermute | solution.py:62
